TPU v7x, 32 devices: a whole 2x2x4 slice. The times are simulated.
32 devices in a mesh: batch: 4 (over z), grid: 8 (over y, x, core).
Axes of the slice: x: 2, y: 2, z: 4, core: 2. Of those that a mesh axis runs over, the one named last changes fastest.
Arguments:
- fields: bfloat16 [1024, 512, 512], P(('batch', 'grid')), parts along dimension 0, may hold values from -18 to 18
- norm_gain: float32 [256], replicated, may hold values from 0.5 to 1.5
- norm_shift: float32 [256], replicated, may hold values from -3 to 3
- first_weight: bfloat16 [2, 8, 32, 32], replicated, may hold values from -0.75 to 0.75
- second_weight: bfloat16 [2, 8, 32, 32], replicated, may hold values from -0.75 to 0.75
- first_bias: float32 [2, 256], replicated, may hold values from -2 to 2
Outputs:
- mixed_fields: bfloat16 [1024, 512, 512], P(('batch', 'grid')), parts along dimension 0
There are 4 independent parts, one for each index of `batch`. A program takes and returns all parts, laid end to end along the dimension named above; an argument that names none is the same for every part. Nothing has to cross between parts.
All inputs are finite; a program needn't handle non-finite values.
Results may differ from a plain program's by a relative error of at most 0.0055.
Values may be sent and summed in bfloat16 or wider, within the bound.
A program may use at most 192 MiB of HBM per device.

v0:
```python
import math

import jax
import jax.numpy as jnp
from jax import lax
from jax.sharding import PartitionSpec as P


def tables(rows, cols):
    half = cols // 2
    col_index = jnp.arange(cols, dtype=jnp.int32)
    mode_index = jnp.arange(half, dtype=jnp.int32)
    angle_w = (col_index[:, None] * mode_index[None, :] % cols).astype(jnp.float32) * (
        2.0 * math.pi / cols
    )
    scale_w = 1.0 / math.sqrt(cols)
    fwd_w = jnp.concatenate(
        [jnp.cos(angle_w) * scale_w, -jnp.sin(angle_w) * scale_w], axis=1
    ).astype(jnp.bfloat16)
    weight_k = jnp.where(mode_index == 0, 1.0, 2.0).astype(jnp.float32)
    inv_w = jnp.concatenate(
        [
            (jnp.cos(angle_w) * weight_k[None, :] * scale_w).T,
            (-jnp.sin(angle_w) * weight_k[None, :] * scale_w).T,
        ],
        axis=0,
    ).astype(jnp.bfloat16)
    row_index = jnp.arange(rows, dtype=jnp.int32)
    angle_h = (row_index[:, None] * row_index[None, :] % rows).astype(jnp.float32) * (
        2.0 * math.pi / rows
    )
    scale_h = 1.0 / math.sqrt(rows)
    cos_h = (jnp.cos(angle_h) * scale_h).astype(jnp.bfloat16)
    sin_h = (jnp.sin(angle_h) * scale_h).astype(jnp.bfloat16)
    return (fwd_w, inv_w, cos_h, sin_h)


def mult(form, left, right):
    return jnp.einsum(form, left, right, preferred_element_type=jnp.float32)


def shrink(values):
    return jnp.maximum(values - 0.01, 0.0) + jnp.minimum(values + 0.01, 0.0)


def mix_modes(real_part, imag_part, first_weight, second_weight, first_bias):
    blocks = first_weight.shape[1]
    width = first_weight.shape[2]
    shape = real_part.shape
    real_blk = real_part.reshape(blocks, width, -1)
    imag_blk = imag_part.reshape(blocks, width, -1)
    bias_blk = first_bias.reshape(2, blocks, width, 1)
    hid_re = jax.nn.relu(
        mult("bio,bim->bom", first_weight[0], real_blk)
        - mult("bio,bim->bom", first_weight[1], imag_blk)
        + bias_blk[0]
    ).astype(jnp.bfloat16)
    hid_im = jax.nn.relu(
        mult("bio,bim->bom", first_weight[0], imag_blk)
        + mult("bio,bim->bom", first_weight[1], real_blk)
        + bias_blk[1]
    ).astype(jnp.bfloat16)
    out_re = mult("bio,bim->bom", second_weight[0], hid_re) - mult(
        "bio,bim->bom", second_weight[1], hid_im
    )
    out_im = mult("bio,bim->bom", second_weight[0], hid_im) + mult(
        "bio,bim->bom", second_weight[1], hid_re
    )
    return (
        shrink(out_re).astype(jnp.bfloat16).reshape(shape),
        shrink(out_im).astype(jnp.bfloat16).reshape(shape),
    )


def per_device(fields, norm_gain, norm_shift, first_weight, second_weight, first_bias):
    local_ch, rows, cols = fields.shape
    half = cols // 2
    groups = lax.axis_size("grid")
    channels = local_ch * groups
    fwd_w, inv_w, cos_h, sin_h = tables(rows, cols)
    values = fields.astype(jnp.float32)
    start = lax.axis_index("grid") * local_ch
    gain_own = lax.dynamic_slice_in_dim(norm_gain, start, local_ch)
    shift_own = lax.dynamic_slice_in_dim(norm_shift, start, local_ch)
    total_sum, total_sq = lax.psum(
        (jnp.sum(values, axis=0), jnp.sum(values * values, axis=0)), "grid"
    )
    mean = total_sum / channels
    var = total_sq / channels - mean * mean
    normed = (
        (values - mean) * lax.rsqrt(var + 1e-05) * gain_own[:, None, None]
        + shift_own[:, None, None]
    ).astype(jnp.bfloat16)
    along_w = (
        mult("chw,wk->chk", normed, fwd_w).astype(jnp.bfloat16).reshape(local_ch, rows, 2, half)
    )
    first_p = mult("kh,chpq->ckpq", cos_h, along_w)
    first_q = mult("kh,chpq->ckpq", sin_h, along_w)
    modes = jnp.stack(
        [
            (first_p[:, :, 0] + first_q[:, :, 1]).astype(jnp.bfloat16),
            (first_p[:, :, 1] - first_q[:, :, 0]).astype(jnp.bfloat16),
        ],
        axis=2,
    )
    spread = lax.all_to_all(modes, "grid", split_axis=1, concat_axis=0, tiled=True)
    shr_re, shr_im = mix_modes(
        spread[:, :, 0], spread[:, :, 1], first_weight, second_weight, first_bias
    )
    gathered = lax.all_to_all(
        jnp.stack([shr_re, shr_im], axis=2), "grid", split_axis=0, concat_axis=1, tiled=True
    )
    back_p = mult("kh,ckpq->chpq", cos_h, gathered)
    back_q = mult("kh,ckpq->chpq", sin_h, gathered)
    back_re = (back_p[:, :, 0] - back_q[:, :, 1]).astype(jnp.bfloat16)
    back_im = (back_p[:, :, 1] + back_q[:, :, 0]).astype(jnp.bfloat16)
    backed = jnp.concatenate([back_re, back_im], axis=2)
    filtered = mult("chk,kw->chw", backed, inv_w)
    return (values + filtered).astype(jnp.bfloat16)


def solution(mesh):
    return jax.shard_map(
        per_device,
        mesh=mesh,
        in_specs=(P(("batch", "grid"), None, None), P(), P(), P(), P(), P()),
        out_specs=P(("batch", "grid"), None, None),
        check_vma=False,
    )
```

profile of v0, /device:TPU:0, one launch (start us, length us, event | category | flops | bytes accessed | tf_op | source)
XLA Modules:
  0.0 897.6 jit_solution(17641309086073437033)
XLA Ops:
  6.5 0.0 all-reduce.3.cloned.1.call-start
  6.5 8.9 convert_reduce_fusion
  15.4 0.0 all-reduce.3.cloned.1.call-update
  15.4 0.0 copy-done.5
  15.4 0.1 dynamic_slice.6
  15.5 0.0 copy-done.6
  15.5 0.1 dynamic_slice.7
  15.6 2.2 multiply_convert_fusion.6
  17.8 62.3 %all-reduce.3.cloned.1.call-done = (f32[512,512]{1,0:T(8,128)}, f32[512,512]{1,0:T(8,128)}) async-done(((f32[512,512]{1,0:T(8,128)}, f32[512,512]{1,0:T(8,128)}), (f32[512,512]{1,0:T(8,128)}, f32[512,512]{1,0:T(8,128)})) %all-reduce.3.cloned.1.call-update) | async-done | bytes 2097168 | tf_op jit(solution)/shard_map/psum | solution.py:85
  80.2 1.8 broadcast_multiply_fusion
  82.0 16.8 %fusion.28 = bf16[32,512,512]{1,2,0:T(8,128)(2,1)} fusion(bf16[32,512,512]{2,1,0:T(8,128)(2,1)} %param.6, f32[32]{0:T(128)S(1)} %dynamic_slice.7, f32[32]{0:T(128)S(1)} %dynamic_slice.6, f32[512,512]{1,0:T(8,128)S(1)} %get-tuple-element.16, f32[512,512]{1,0:T(8,128)S(1)} %get-tuple-element.15, bf16[512,256]{0,1:T(8,128)(2,1)S(1)} %get-tuple-element.19, ...), kind=kOutput, calls=%fused_computation.48 | convolution fusion | flops 8649703424 | bytes 36176128 | tf_op jit(solution)/shard_map/chw,wk->chk/dot_general | solution.py:39
  98.8 24.6 %convolution_bitcast_fusion.2 = f32[32,512,2,256]{1,3,2,0:T(8,128)} fusion(bf16[32,512,2,256]{1,3,2,0:T(8,128)(2,1)} %bitcast.117), kind=kOutput, calls=%fused_computation.46 | convolution fusion | flops 8594128896 | bytes 50331648 | tf_op jit(solution)/shard_map/kh,chpq->ckpq/dot_general | solution.py:39
  123.4 24.6 %convolution_bitcast_fusion.3 = f32[32,512,2,256]{1,3,2,0:T(8,128)} fusion(bf16[32,512,2,256]{1,3,2,0:T(8,128)(2,1)} %bitcast.118), kind=kOutput, calls=%fused_computation.47 | convolution fusion | flops 8594128896 | bytes 50331648 | tf_op jit(solution)/shard_map/kh,chpq->ckpq/dot_general | solution.py:39
  148.0 25.6 %fusion.18 = (bf16[32,512,1,256]{1,3,2,0:T(8,128)(2,1)S(1)}, bf16[32,512,1,256]{1,3,2,0:T(8,128)(2,1)}) fusion(f32[32,512,2,256]{1,3,2,0:T(8,128)} %convolution_bitcast_fusion.2, f32[32,512,2,256]{1,3,2,0:T(8,128)} %convolution_bitcast_fusion.3), kind=kLoop, calls=%fused_computation.31 | loop fusion | flops 16777216 | bytes 83886080 | tf_op jit(solution)/shard_map/convert_element_type | solution.py:101
  173.6 10.5 %pad_maximum_fusion = bf16[32,512,2,256]{1,3,2,0:T(8,128)(2,1)} fusion(bf16[32,512,1,256]{1,3,2,0:T(8,128)(2,1)} %get-tuple-element.12, bf16[32,512,1,256]{1,3,2,0:T(8,128)(2,1)S(1)} %get-tuple-element.11), kind=kLoop, calls=%fused_computation.32 | loop fusion | flops 8388608 | bytes 33554432 | tf_op jit(solution)/shard_map/stack | solution.py:99
  184.1 41.4 %copy.43 = bf16[32,512,2,256]{3,2,0,1:T(2,128)(2,1)} copy(bf16[32,512,2,256]{1,3,2,0:T(8,128)(2,1)} %pad_maximum_fusion) | data formatting | bytes 33554432 | tf_op jit(solution)/shard_map/stack | solution.py:99
  225.4 5.9 all-to-all-start
  231.3 0.0 copy-done.4
  231.3 0.1 add.121
  231.4 0.1 add.125
  231.5 183.7 %all-to-all-done = bf16[32,512,2,256]{3,2,0,1:T(2,128)(2,1)} async-done(((bf16[32,512,2,256]{3,2,0,1:T(2,128)(2,1)}), bf16[32,512,2,256]{3,2,0,1:T(2,128)(2,1)}, u32[]{:S(2)}, u32[]{:S(2)}) %all-to-all-start) | async-done | bytes 16777248 | tf_op jit(solution)/shard_map/all_to_all | solution.py:106
  415.2 10.4 %copy.44 = bf16[32,512,2,256]{3,1,2,0:T(8,128)(2,1)S(1)} copy(bf16[32,512,2,256]{3,2,0,1:T(2,128)(2,1)} %all-to-all-done) | data formatting | bytes 33554432 | tf_op jit(solution)/shard_map/all_to_all | solution.py:106
  425.7 2.3 copy.45
  428.0 6.4 fusion.104
  434.4 13.5 %reshape_squeeze.6 = bf16[8,32,16384]{2,1,0:T(8,128)(2,1)} reshape(bf16[256,64,1,256]{3,1,2,0:T(8,128)(2,1)} %get-tuple-element.13) | data formatting | bytes 16777216 | tf_op jit(solution)/shard_map/reshape;squeeze | solution.py:50
  447.9 13.5 %reshape_squeeze.7 = bf16[8,32,16384]{2,1,0:T(8,128)(2,1)} reshape(bf16[256,64,1,256]{3,1,2,0:T(8,128)(2,1)} %get-tuple-element.14) | data formatting | bytes 16777216 | tf_op jit(solution)/shard_map/reshape;squeeze | solution.py:51
  461.4 11.6 %fusion.72 = f32[8,16384,32]{1,2,0:T(8,128)} fusion(bf16[8,32,16384]{2,1,0:T(8,128)(2,1)} %reshape_squeeze.6, bf16[2,8,32,32]{3,2,1,0:T(8,128)(2,1)S(1)} %copy-done.3), kind=kOutput, calls=%fused_computation.105 | convolution fusion | flops 268435456 | bytes 25231360 | tf_op jit(solution)/shard_map/bio,bim->bom/dot_general | solution.py:39
  473.0 0.0 copy-done.1
  473.0 7.6 fusion.70
  480.7 0.0 copy-start.2
  480.7 13.9 %fusion.11 = bf16[8,16384,32]{1,2,0:T(8,128)(2,1)} fusion(f32[8,16384,32]{1,2,0:T(8,128)} %fusion.72, bf16[8,32,16384]{2,1,0:T(8,128)(2,1)} %reshape_squeeze.7, f32[8,32]{1,0:T(8,128)S(1)} %add.121, bf16[2,8,32,32]{3,2,1,0:T(8,128)(2,1)S(1)} %copy-done.3), kind=kOutput, calls=%fused_computation.19 | convolution fusion | flops 285212672 | bytes 33624064 | tf_op jit(solution)/shard_map/bio,bim->bom/dot_general | solution.py:39
  494.6 11.5 %fusion.66 = f32[8,16384,32]{1,2,0:T(8,128)} fusion(bf16[8,16384,32]{1,2,0:T(8,128)(2,1)} %fusion.11, bf16[2,8,32,32]{3,2,1,0:T(8,128)(2,1)S(1)} %copy-done.2), kind=kOutput, calls=%fused_computation.99 | convolution fusion | flops 268435456 | bytes 25231360 | tf_op jit(solution)/shard_map/bio,bim->bom/dot_general | solution.py:39
  506.1 13.9 %fusion.10 = bf16[8,16384,32]{1,2,0:T(8,128)(2,1)} fusion(f32[8,16384,32]{1,2,0:T(8,128)} %fusion.70, bf16[8,32,16384]{2,1,0:T(8,128)(2,1)} %reshape_squeeze.6, f32[8,32]{1,0:T(8,128)S(1)} %add.125, bf16[2,8,32,32]{3,2,1,0:T(8,128)(2,1)S(1)} %copy-done.3), kind=kOutput, calls=%fused_computation.18 | convolution fusion | flops 285212672 | bytes 33624064 | tf_op jit(solution)/shard_map/bio,bim->bom/dot_general | solution.py:39
  520.0 12.1 %fusion.64 = f32[8,16384,32]{1,2,0:T(8,128)} fusion(bf16[8,16384,32]{1,2,0:T(8,128)(2,1)} %fusion.10, bf16[2,8,32,32]{3,2,1,0:T(8,128)(2,1)S(1)} %copy-done.2), kind=kOutput, calls=%fused_computation.97 | convolution fusion | flops 268435456 | bytes 25231360 | tf_op jit(solution)/shard_map/bio,bim->bom/dot_general | solution.py:39
  532.0 10.3 %add_convert_fusion.1 = bf16[8,16384,32]{1,2,0:T(8,128)(2,1)} fusion(f32[8,16384,32]{1,2,0:T(8,128)} %fusion.66, bf16[8,16384,32]{1,2,0:T(8,128)(2,1)S(1)} %copy-done, bf16[2,8,32,32]{3,2,1,0:T(8,128)(2,1)S(1)} %copy-done.2), kind=kOutput, calls=%fused_computation.40 | convolution fusion | flops 297795584 | bytes 33619968 | tf_op jit(solution)/shard_map/bio,bim->bom/dot_general | solution.py:39
  542.3 9.4 %copy.71 = bf16[32,8,64,256]{3,2,1,0:T(8,128)(2,1)} copy(bf16[32,8,64,256]{3,1,2,0:T(8,128)(2,1)} %bitcast.123) | data formatting | bytes 16777216
  551.7 13.2 %add_convert_fusion = bf16[8,16384,32]{1,2,0:T(8,128)(2,1)} fusion(f32[8,16384,32]{1,2,0:T(8,128)} %fusion.64, bf16[8,16384,32]{1,2,0:T(8,128)(2,1)} %fusion.11, bf16[2,8,32,32]{3,2,1,0:T(8,128)(2,1)S(1)} %copy-done.2), kind=kOutput, calls=%fused_computation.39 | convolution fusion | flops 297795584 | bytes 33619968 | tf_op jit(solution)/shard_map/bio,bim->bom/dot_general | solution.py:39
  564.9 9.4 %copy.72 = bf16[32,8,64,256]{3,2,1,0:T(8,128)(2,1)} copy(bf16[32,8,64,256]{3,1,2,0:T(8,128)(2,1)} %bitcast.124) | data formatting | bytes 16777216
  574.3 13.8 %pad_maximum_fusion.1 = bf16[256,64,2,256]{3,1,2,0:T(8,128)(2,1)} fusion(bf16[256,64,1,256]{3,1,2,0:T(8,128)(2,1)} %bitcast.126, bf16[256,64,1,256]{3,1,2,0:T(8,128)(2,1)} %bitcast.125), kind=kLoop, calls=%fused_computation.33 | loop fusion | flops 8388608 | bytes 33554432 | tf_op jit(solution)/shard_map/stack | solution.py:111
  588.2 5.9 all-to-all-start.1
  594.1 2.3 multiply_convert_fusion.3
  596.4 181.6 %all-to-all-done.1 = bf16[256,64,2,256]{3,1,2,0:T(8,128)(2,1)} async-done(((bf16[256,64,2,256]{3,1,2,0:T(8,128)(2,1)}), bf16[256,64,2,256]{3,1,2,0:T(8,128)(2,1)}, u32[]{:S(2)}, u32[]{:S(2)}) %all-to-all-start.1) | async-done | bytes 16777248 | tf_op jit(solution)/shard_map/all_to_all | solution.py:110
  778.0 14.2 %copy.52 = bf16[32,8,64,2,256]{4,2,1,3,0:T(8,128)(2,1)} copy(bf16[32,8,64,2,256]{4,2,3,0,1:T(8,128)(2,1)} %bitcast.20) | data formatting | bytes 33554432 | tf_op jit(solution)/shard_map/all_to_all | solution.py:110
  792.2 22.1 %convolution_bitcast_fusion = f32[32,512,2,256]{1,3,0,2:T(8,128)} fusion(bf16[32,512,2,256]{3,1,2,0:T(8,128)(2,1)} %bitcast.119), kind=kOutput, calls=%fused_computation.20 | convolution fusion | flops 8594128896 | bytes 50331648 | tf_op jit(solution)/shard_map/kh,ckpq->chpq/dot_general | solution.py:39
  814.3 24.7 %convolution_bitcast_fusion.1 = f32[32,512,2,256]{1,3,2,0:T(8,128)} fusion(bf16[32,512,2,256]{3,1,2,0:T(8,128)(2,1)} %bitcast.120), kind=kOutput, calls=%fused_computation.45 | convolution fusion | flops 8594128896 | bytes 50331648 | tf_op jit(solution)/shard_map/kh,ckpq->chpq/dot_general | solution.py:39
  839.0 15.1 %fusion.33 = bf16[32,512,256]{1,2,0:T(8,128)(2,1)} fusion(f32[32,512,2,256]{1,3,0,2:T(8,128)} %convolution_bitcast_fusion, f32[32,512,2,256]{1,3,2,0:T(8,128)} %convolution_bitcast_fusion.1), kind=kLoop, calls=%fused_computation.49 | loop fusion | flops 8388608 | bytes 41943040 | tf_op jit(solution)/shard_map/convert_element_type | solution.py:115
  854.1 15.1 %fusion.34 = bf16[32,512,256]{1,2,0:T(8,128)(2,1)} fusion(f32[32,512,2,256]{1,3,0,2:T(8,128)} %convolution_bitcast_fusion, f32[32,512,2,256]{1,3,2,0:T(8,128)} %convolution_bitcast_fusion.1), kind=kLoop, calls=%fused_computation.50 | loop fusion | flops 8388608 | bytes 41943040 | tf_op jit(solution)/shard_map/convert_element_type | solution.py:116
  869.2 21.3 %fusion.5 = bf16[32,512,512]{2,1,0:T(8,128)(2,1)} fusion(bf16[32,512,512]{2,1,0:T(8,128)(2,1)} %param.6, bf16[32,512,256]{1,2,0:T(8,128)(2,1)} %fusion.34, bf16[32,512,256]{1,2,0:T(8,128)(2,1)} %fusion.33, bf16[256,512]{1,0:T(8,128)(2,1)S(1)} %get-tuple-element.18, bf16[256,512]{1,0:T(8,128)(2,1)S(1)} %get-tuple-element.17), kind=kOutput, calls=%fused_computation.9 | convolution fusion | flops 8649703424 | bytes 50855936 | tf_op jit(solution)/shard_map/chk,kw->chw/dot_general | solution.py:39
  (11 shorter events, 0.0 us)
Async XLA Ops:
  6.5 8.9 copy-start.5
  6.5 9.0 %copy-start.6 = (f32[256]{0:T(256)S(1)}, f32[256]{0:T(256)}, u32[]{:S(2)}) copy-start(f32[256]{0:T(256)} %param.8) | copy-start | bytes 3076
  6.5 73.6 %all-reduce.3.cloned.1.call-start = ((), (), s32[]{:S(2)}) async-start(), calls=%async_computation.2 | async-start | bytes 4194304 | tf_op jit(solution)/shard_map/psum | solution.py:85
  225.4 5.9 copy-start.4
  225.4 189.8 %all-to-all-start = ((bf16[32,512,2,256]{3,2,0,1:T(2,128)(2,1)}), bf16[32,512,2,256]{3,2,0,1:T(2,128)(2,1)}, u32[]{:S(2)}, u32[]{:S(2)}) async-start(bf16[32,512,2,256]{3,2,0,1:T(2,128)(2,1)} %copy.43), calls=%async_computation | async-start | bytes 33554432 | tf_op jit(solution)/shard_map/all_to_all | solution.py:106
  434.4 27.0 %copy-start.3 = (bf16[2,8,32,32]{3,2,1,0:T(8,128)(2,1)S(1)}, bf16[2,8,32,32]{3,2,1,0:T(8,128)(2,1)}, u32[]{:S(2)}) copy-start(bf16[2,8,32,32]{3,2,1,0:T(8,128)(2,1)} %param.9) | copy-start | bytes 98308
  461.4 11.6 %copy-start.1 = (bf16[8,32,16384]{2,1,0:T(8,128)(2,1)S(1)}, bf16[8,32,16384]{2,1,0:T(8,128)(2,1)}, u32[]{:S(2)}) copy-start(bf16[8,32,16384]{2,1,0:T(8,128)(2,1)} %reshape_squeeze.7) | copy-start | bytes 25165828
  480.7 13.9 %copy-start.2 = (bf16[2,8,32,32]{3,2,1,0:T(8,128)(2,1)S(1)}, bf16[2,8,32,32]{3,2,1,0:T(8,128)(2,1)}, u32[]{:S(2)}) copy-start(bf16[2,8,32,32]{3,2,1,0:T(8,128)(2,1)} %param.10) | copy-start | bytes 98308
  520.0 12.1 %copy-start = (bf16[8,16384,32]{1,2,0:T(8,128)(2,1)S(1)}, bf16[8,16384,32]{1,2,0:T(8,128)(2,1)}, u32[]{:S(2)}) copy-start(bf16[8,16384,32]{1,2,0:T(8,128)(2,1)} %fusion.10) | copy-start | bytes 25165828
  588.2 189.9 %all-to-all-start.1 = ((bf16[256,64,2,256]{3,1,2,0:T(8,128)(2,1)}), bf16[256,64,2,256]{3,1,2,0:T(8,128)(2,1)}, u32[]{:S(2)}, u32[]{:S(2)}) async-start(bf16[256,64,2,256]{3,1,2,0:T(8,128)(2,1)} %pad_maximum_fusion.1), calls=%async_computation.1 | async-start | bytes 33554432 | tf_op jit(solution)/shard_map/all_to_all | solution.py:110
Sparse Core Ops, SparseCore 0:
  15.6 64.5 all-reduce.2
where the time goes:
time: 909 us; the launch traced here: 898 us
  waiting for transfers between devices  428 us (47%)
  matrix products  228 us (25%)
  local copies, waits for them, and re-layouts  121 us (13%)
  other arithmetic  95.3 us (10%)
  between operations  13.7 us (2%)
  starting transfers between devices  11.8 us (1%)
    dot_general x14, matrix products, mult(): return jnp.einsum(form, left, right, preferred_element_type=jnp.float32)  228 us
    all_to_all x1, waiting for transfers between devices, per_device(): lax.all_to_all(modes, 'grid', split_axis=1, concat_axis=0, tiled=True)  184 us
    all_to_all x1, waiting for transfers between devices, per_device(): lax.all_to_all(jnp.stack([shr_re, shr_im], axis=2), 'grid', split_axis=0,...  182 us
    psum x1, waiting for transfers between devices, per_device(): lax.psum((jnp.sum(values, axis=0), jnp.sum(values * values, axis=0)), 'gr...  62.3 us
    another operation x1, local copies, waits for them, and re-layouts, per_device(): jnp.stack([(first_p[:, :, 0] + first_q[:, :, 1]).astype(jnp.bfloat16), (f...  41.4 us
    convert_element_type x1, other arithmetic, per_device(): (first_p[:, :, 0] + first_q[:, :, 1]).astype(jnp.bfloat16)  25.6 us
    unnamed x16, local copies, waits for them, and re-layouts  18.8 us
  transfers between devices with their start and end apart: 3, of which 3 were waited for; matrix products, arithmetic and copies ran while one was open for 1% of the time, Pallas kernels for 0%

commit v1 on v0

--- a/solution.py
+++ b/solution.py
@@ -3,6 +3,8 @@
 import jax
 import jax.numpy as jnp
 from jax import lax
+from jax.experimental import pallas as pl
+from jax.experimental.pallas import tpu as pltpu
 from jax.sharding import PartitionSpec as P
 
 
@@ -118,10 +120,222 @@
     filtered = mult("chk,kw->chw", backed, inv_w)
     return (values + filtered).astype(jnp.bfloat16)
 
+SUB = 8
+
+
+def half_tables(cos_h, sin_h):
+    rows = cos_h.shape[0]
+    mid = rows // 2
+    low = jnp.concatenate([cos_h[:mid], cos_h[mid : mid + 1], sin_h[1:mid]], axis=0)
+    picked = jnp.arange(mid, dtype=jnp.int32)
+    swap = (jnp.where(picked == 0, 0, mid - picked)[:, None] == picked[None, :]).astype(
+        jnp.bfloat16
+    )
+    order = lambda t: jnp.concatenate(
+        [t[:, :mid], t[:, mid : mid + 1], t[:, mid + 1 :][:, ::-1]], axis=1
+    )
+    return low, order(low), swap
+
+
+def spread_weight(weight):
+    eye = jnp.eye(SUB, dtype=weight.dtype)
+    real = jnp.einsum("bio,st->bosit", weight[0], eye)
+    imag = jnp.einsum("bio,st->bosit", weight[1], eye)
+    blocks, width = weight.shape[1], weight.shape[2]
+    size = width * SUB
+    real = real.reshape(blocks, size, size)
+    imag = imag.reshape(blocks, size, size)
+    return jnp.concatenate(
+        [jnp.concatenate([real, -imag], axis=2), jnp.concatenate([imag, real], axis=2)],
+        axis=1,
+    )
+
+
+def split_rows(total, sign):
+    mid, half = total.shape[0] // 2, total.shape[1] // 2
+    p_re, p_im = total[:mid, :half], total[:mid, half:]
+    q_re, q_im = total[mid:, :half], total[mid:, half:]
+    edge = lax.broadcasted_iota(jnp.int32, (mid, half), 0) == 0
+    t_re = jnp.where(edge, 0.0, q_re)
+    t_im = jnp.where(edge, 0.0, q_im)
+    if sign < 0:
+        t_re, t_im = -t_re, -t_im
+    plus = (p_re + t_im, p_im - t_re)
+    minus = (
+        jnp.where(edge, q_re, p_re - t_im),
+        jnp.where(edge, q_im, p_im + t_re),
+    )
+    return plus, minus
+
+
+def forward_kernel(x_ref, mean_ref, rstd_ref, gain_ref, shift_ref, fw_ref, fh_ref, out_ref):
+    count, rows, cols = x_ref.shape
+    mid, half = rows // 2, cols // 2
+    step = pl.program_id(0)
+    for n in range(count):
+        gain = gain_ref[step * count + n]
+        shift = shift_ref[step * count + n]
+        values = x_ref[n].astype(jnp.float32)
+        normed = ((values - mean_ref[...]) * rstd_ref[...] * gain + shift).astype(jnp.bfloat16)
+        along = jnp.dot(normed, fw_ref[...], preferred_element_type=jnp.float32).astype(
+            jnp.bfloat16
+        )
+        total = jnp.dot(fh_ref[...], along, preferred_element_type=jnp.float32)
+        plus, minus = split_rows(total, 1)
+        for place, pair in ((0, plus), (mid, minus)):
+            for side in range(2):
+                out_ref[n, place : place + mid, side * half : (side + 1) * half] = pair[
+                    side
+                ].astype(jnp.bfloat16)
+
+
+def mix_kernel(x_ref, w1_ref, w2_ref, bias_ref, out_ref):
+    width, depth, cols = x_ref.shape
+    half = cols // 2
+    size = width * SUB
+    for g in range(depth // (2 * SUB)):
+        base = g * 2 * SUB
+        values = x_ref[:, base : base + 2 * SUB, :].astype(jnp.float32)
+        parts = []
+        for s in range(2):
+            flat = values[:, s * SUB : (s + 1) * SUB, :].reshape(size, cols).astype(jnp.bfloat16)
+            both = jnp.concatenate([flat[:, :half], flat[:, half:]], axis=0)
+            hid = jnp.dot(w1_ref[0], both, preferred_element_type=jnp.float32)
+            hid = jnp.maximum(hid + bias_ref[0], 0.0).astype(jnp.bfloat16)
+            mixed = shrink(jnp.dot(w2_ref[0], hid, preferred_element_type=jnp.float32))
+            parts.append(mixed.reshape(2, width, SUB, half))
+        for side in range(2):
+            out_ref[:, base : base + 2 * SUB, side * half : (side + 1) * half] = (
+                jnp.concatenate([parts[0][side], parts[1][side]], axis=1).astype(jnp.bfloat16)
+            )
+
+
+def backward_kernel(x_ref, s_ref, bh_ref, swap_ref, iw_ref, out_ref):
+    count, rows, cols = x_ref.shape
+    mid = rows // 2
+    for n in range(count):
+        total = jnp.dot(bh_ref[...], s_ref[n], preferred_element_type=jnp.float32)
+        plus, minus = split_rows(total, -1)
+        upper = jnp.concatenate([t.astype(jnp.bfloat16) for t in plus], axis=1)
+        lower = jnp.concatenate([t.astype(jnp.bfloat16) for t in minus], axis=1)
+        lower = jnp.dot(swap_ref[...], lower, preferred_element_type=jnp.float32).astype(
+            jnp.bfloat16
+        )
+        for place, part in ((0, upper), (mid, lower)):
+            filtered = jnp.dot(part, iw_ref[...], preferred_element_type=jnp.float32)
+            out_ref[n, place : place + mid, :] = (
+                x_ref[n, place : place + mid, :].astype(jnp.float32) + filtered
+            ).astype(jnp.bfloat16)
+
+
+def whole_spec(array):
+    zeros = (0,) * array.ndim
+    return pl.BlockSpec(array.shape, lambda i: zeros)
+
+
+def per_device_local(fields, norm_gain, norm_shift, first_weight, second_weight, first_bias):
+    local_ch, rows, cols = fields.shape
+    half = cols // 2
+    width = first_weight.shape[2]
+    groups = lax.axis_size("grid")
+    channels = local_ch * groups
+    own_blocks = local_ch // width
+    values = fields.astype(jnp.float32)
+    total_sum, total_sq = lax.psum(
+        (jnp.sum(values, axis=0), jnp.sum(values * values, axis=0)), "grid"
+    )
+    mean = total_sum / channels
+    rstd = lax.rsqrt(total_sq / channels - mean * mean + 1e-05)
+    fwd_w, inv_w, cos_h, sin_h = tables(rows, cols)
+    low, ordered, swap = half_tables(cos_h, sin_h)
+    place = lax.axis_index("grid")
+    take = lambda a, size, axis: lax.dynamic_slice_in_dim(a, place * size, size, axis)
+    gain_own = take(norm_gain, local_ch, 0)
+    shift_own = take(norm_shift, local_ch, 0)
+    first_own = spread_weight(take(first_weight, own_blocks, 1))
+    second_own = spread_weight(take(second_weight, own_blocks, 1))
+    bias_own = take(first_bias, local_ch, 1).reshape(2, own_blocks, width)
+    bias_own = jnp.repeat(
+        bias_own.transpose(1, 0, 2).reshape(own_blocks, 2 * width, 1), SUB, axis=1
+    )
+    size = 2 * width * SUB
+    per = 2 if local_ch % 2 == 0 else 1
+    params = pltpu.CompilerParams(
+        dimension_semantics=("arbitrary",), vmem_limit_bytes=60 * 1024 * 1024
+    )
+    image = jax.ShapeDtypeStruct(fields.shape, jnp.bfloat16)
+    image_spec = pl.BlockSpec((per, rows, cols), lambda i: (i, 0, 0))
+    smem = pl.BlockSpec(memory_space=pltpu.SMEM)
+    cost = lambda flops: pl.CostEstimate(
+        flops=flops, bytes_accessed=4 * fields.size, transcendentals=0
+    )
+    modes = pl.pallas_call(
+        forward_kernel,
+        grid=(local_ch // per,),
+        out_shape=image,
+        in_specs=[
+            image_spec,
+            whole_spec(mean),
+            whole_spec(rstd),
+            smem,
+            smem,
+            whole_spec(fwd_w),
+            whole_spec(low),
+        ],
+        out_specs=image_spec,
+        compiler_params=params,
+        cost_estimate=cost(2 * fields.size * (rows + cols)),
+        name="forward",
+    )(fields, mean, rstd, gain_own, shift_own, fwd_w, low)
+    depth = 4 * SUB
+    mode_spec = pl.BlockSpec((width, depth, cols), lambda b, i: (b, i, 0))
+    weight_spec = pl.BlockSpec((1, size, size), lambda b, i: (b, 0, 0))
+    mixed = pl.pallas_call(
+        mix_kernel,
+        grid=(own_blocks, rows // depth),
+        out_shape=image,
+        in_specs=[
+            mode_spec,
+            weight_spec,
+            weight_spec,
+            pl.BlockSpec((1, size, 1), lambda b, i: (b, 0, 0)),
+        ],
+        out_specs=mode_spec,
+        compiler_params=pltpu.CompilerParams(
+            dimension_semantics=("arbitrary", "arbitrary"), vmem_limit_bytes=60 * 1024 * 1024
+        ),
+        cost_estimate=cost(2 * fields.size * size),
+        name="mix",
+    )(modes, first_own, second_own, bias_own)
+    return pl.pallas_call(
+        backward_kernel,
+        grid=(local_ch // per,),
+        out_shape=image,
+        in_specs=[
+            image_spec,
+            image_spec,
+            whole_spec(ordered),
+            whole_spec(swap),
+            whole_spec(inv_w),
+        ],
+        out_specs=image_spec,
+        compiler_params=params,
+        cost_estimate=cost(2 * fields.size * (rows + cols)),
+        name="backward",
+    )(fields, mixed, ordered, swap, inv_w)
+
+
+def per_device_any(fields, norm_gain, norm_shift, first_weight, second_weight, first_bias):
+    local_ch, rows, cols = fields.shape
+    whole_blocks = local_ch % first_weight.shape[2] == 0
+    tiled = rows % 64 == 0 and cols % 256 == 0 and rows * cols <= 512 * 1024
+    chosen = per_device_local if whole_blocks and tiled else per_device
+    return chosen(fields, norm_gain, norm_shift, first_weight, second_weight, first_bias)
+
 
 def solution(mesh):
     return jax.shard_map(
-        per_device,
+        per_device_any,
         mesh=mesh,
         in_specs=(P(("batch", "grid"), None, None), P(), P(), P(), P(), P()),
         out_specs=P(("batch", "grid"), None, None),

time: 909 us -> 180 us (0.20)
  waiting for transfers between devices: 428 us -> 24.2 us
  matrix products: 228 us -> 0 us
  local copies, waits for them, and re-layouts: 121 us -> 20.8 us
  Pallas kernels: 0 us -> 87.4 us
  other arithmetic: 95.3 us -> 31.7 us
  starting transfers between devices: 11.8 us -> 0.01 us
    all_to_all x2 -> x0, waiting for transfers between devices: 365 us -> none  [the longest x1 184 us: per_device(): lax.all_to_all(modes, 'grid', split_axis=1, concat_axis=0, tiled=True)]
    dot_general x14 -> x0, matrix products: 228 us -> none  [mult(): return jnp.einsum(form, left, right, preferred_element_type=jnp.float32)]
    pallas_call x0 -> x3, Pallas kernels: none -> 87.4 us  [the longest x1 31.8 us: per_device_local(): pl.pallas_call(backward_kernel, grid=(local_ch // per,), out_shape=image,...]
    another operation x3 -> x5, local copies, waits for them, and re-layouts: 68.3 us -> 1.16 us  [the longest x1 41.4 us: per_device(): jnp.stack([(first_p[:, :, 0] + first_q[:, :, 1]).astype(jnp.bfloat16), (f...]
    convert_element_type x3, other arithmetic: 55.7 us -> 4.35 us  [the longest x1 1.8 us: tables(): cos_h = (jnp.cos(angle_h) * scale_h).astype(jnp.bfloat16)]
    psum x1, waiting for transfers between devices: 62.3 us -> 24.2 us  [per_device_local(): lax.psum((jnp.sum(values, axis=0), jnp.sum(values * values, axis=0)), 'gr...]
    all_to_all x3 -> x0, local copies, waits for them, and re-layouts: 26.9 us -> none  [the longest x1 14.2 us: per_device(): lax.all_to_all(jnp.stack([shr_re, shr_im], axis=2), 'grid', split_axis=0,...]
    another operation x4 -> x3, other arithmetic: 28.8 us -> 4.45 us  [the longest x1 13.8 us: per_device(): jnp.stack([shr_re, shr_im], axis=2)]
  transfers between devices with their start and end apart: 3 -> 1, of which waited for: 3 -> 1; matrix products, arithmetic and copies ran while one was open for 1% -> 23% of each run, Pallas kernels for 0% -> 0%
where the time goes in v1:
time: 180 us; the launch traced here: 178 us
  Pallas kernels  87.4 us (49%)
  other arithmetic  31.7 us (18%)
  waiting for transfers between devices  24.2 us (13%)
  local copies, waits for them, and re-layouts  20.8 us (12%)
  between operations  13.5 us (8%)
    pallas_call x1, Pallas kernels, per_device_local(): pl.pallas_call(backward_kernel, grid=(local_ch // per,), out_shape=image,...  31.8 us
    pallas_call x1, Pallas kernels, per_device_local(): pl.pallas_call(mix_kernel, grid=(own_blocks, rows // depth), out_shape=im...  28.1 us
    pallas_call x1, Pallas kernels, per_device_local(): pl.pallas_call(forward_kernel, grid=(local_ch // per,), out_shape=image,...  27.5 us
    psum x1, waiting for transfers between devices, per_device_local(): lax.psum((jnp.sum(values, axis=0), jnp.sum(values * values, axis=0)), 'gr...  24.2 us
    reduce_sum x1, other arithmetic, per_device_local(): jnp.sum(values * values, axis=0)  8.91 us
    reshape x2, local copies, waits for them, and re-layouts, spread_weight(): real = real.reshape(blocks, size, size)  8.24 us
    reshape x2, local copies, waits for them, and re-layouts, spread_weight(): imag = imag.reshape(blocks, size, size)  8.15 us
    another operation x3, other arithmetic  4.45 us
  transfers between devices with their start and end apart: 1, of which 1 were waited for; matrix products, arithmetic and copies ran while one was open for 23% of the time, Pallas kernels for 0%

profile of v1, /device:TPU:0, one launch (start us, length us, event | category | flops | bytes accessed | tf_op | source)
XLA Modules:
  0.0 177.6 jit_solution(6023393526225915145)
XLA Ops:
  6.5 0.0 copy-start
  6.5 0.0 all-reduce.3.cloned.1.call-start
  6.5 8.9 %fusion = (f32[512,512]{1,0:T(8,128)}, f32[512,512]{1,0:T(8,128)}) fusion(bf16[32,512,512]{2,1,0:T(8,128)(2,1)} %x_ref.3), kind=kLoop, calls=%fused_computation.2 | loop fusion | flops 33030144 | bytes 18874368 | tf_op jit(solution)/shard_map/reduce_sum | solution.py:245
  15.4 0.0 all-reduce.3.cloned.1.call-update
  15.5 0.5 fusion.3
  16.0 1.8 %fusion.8 = bf16[257,512]{1,0:T(8,128)(2,1)S(1)} fusion(f32[512,512]{1,0:T(8,128)S(1)} %fusion.3), kind=kLoop, calls=%fused_computation.30 | loop fusion | flops 263168 | bytes 789504 | tf_op jit(solution)/shard_map/convert_element_type | solution.py:35
  17.8 1.8 %fusion.16 = bf16[255,512]{1,0:T(8,128)(2,1)S(1)} fusion(f32[512,512]{1,0:T(8,128)S(1)} %fusion.3), kind=kLoop, calls=%fused_computation.39 | loop fusion | flops 261120 | bytes 783360 | tf_op jit(solution)/shard_map/convert_element_type | solution.py:36
  19.6 2.2 %multiply_convert_fusion.2 = (bf16[512,256]{1,0:T(8,128)(2,1)S(1)}, bf16[512,256]{1,0:T(8,128)(2,1)S(1)}) fusion(), kind=kLoop, calls=%fused_computation.49 | loop fusion | flops 2490368 | bytes 524288 | tf_op jit(solution)/shard_map/convert.7
  21.8 0.9 pad_maximum_fusion.fh_ref
  22.7 0.2 fusion.24
  22.9 0.1 fusion.23
  23.0 0.8 dynamic-slice_bitcast_fusion
  23.8 0.1 copy.11
  23.9 0.1 copy.12
  23.9 0.1 copy.13
  24.0 0.1 copy.14
  24.1 3.1 %multiply_bitcast_fusion = (bf16[1,32,8,32,8]{4,3,2,1,0:T(8,128)(2,1)}, bf16[1,32,8,32,8]{4,3,2,1,0:T(8,128)(2,1)}, bf16[1,32,8,32,8]{4,3,2,1,0:T(8,128)(2,1)S(1)}, bf16[1,32,8,32,8]{4,3,2,1,0:T(8,128)(2,1)}) fusion(bf16[32,32]{0,1:T(8,128)(2,1)S(1)} %copy.14, bf16[8,8]{1,0:T(8,128)(2,1)S(1)} %fusion.26, bf16[32,32]{0,1:T(8,128)(2,1)S(1)} %copy.12, ...), kind=kLoop, calls=%fused_computation.3 | loop fusion | flops 262144 | bytes 532608 | tf_op jit(solution)/shard_map/bio,st->bosit/transpose | solution.py:143
  27.2 4.1 %reshape.77 = bf16[1,256,256]{2,1,0:T(8,128)(2,1)S(1)} reshape(bf16[1,32,8,32,8]{4,3,2,1,0:T(8,128)(2,1)} %get-tuple-element.16) | data formatting | bytes 262144 | tf_op jit(solution)/shard_map/reshape | solution.py:147
  31.3 0.7 neg.30
  31.9 4.7 %reshape.75 = bf16[1,256,256]{2,1,0:T(8,128)(2,1)} reshape(bf16[1,32,8,32,8]{4,3,2,1,0:T(8,128)(2,1)} %get-tuple-element.18) | data formatting | bytes 262144 | tf_op jit(solution)/shard_map/reshape | solution.py:146
  36.6 4.1 %reshape.81 = bf16[1,256,256]{2,1,0:T(8,128)(2,1)S(1)} reshape(bf16[1,32,8,32,8]{4,3,2,1,0:T(8,128)(2,1)} %get-tuple-element.15) | data formatting | bytes 262144 | tf_op jit(solution)/shard_map/reshape | solution.py:147
  40.7 0.7 neg.31
  41.4 3.6 %reshape.79 = bf16[1,256,256]{2,1,0:T(8,128)(2,1)} reshape(bf16[1,32,8,32,8]{4,3,2,1,0:T(8,128)(2,1)S(1)} %get-tuple-element.17) | data formatting | bytes 262144 | tf_op jit(solution)/shard_map/reshape | solution.py:146
  45.0 0.0 copy-done.4
  45.0 0.7 dynamic_slice.15.gain_ref
  45.6 0.0 copy-done.5
  45.6 0.6 dynamic_slice.16.shift_ref
  46.2 0.0 copy-done
  46.2 0.1 constant_dynamic-slice_fusion
  46.3 0.1 reshape_transpose_reshape.3
  46.4 0.1 broadcast_in_dim.14
  46.5 0.8 broadcast_in_dim.27.bias_ref
  47.3 0.8 reverse
  48.1 0.1 slice.64
  48.3 1.9 %maximum_maximum_fusion.w1_ref = bf16[1,512,512]{2,1,0:T(8,128)(2,1)} fusion(bf16[1,256,256]{2,1,0:T(8,128)(2,1)} %reshape.75, bf16[1,256,256]{2,1,0:T(8,128)(2,1)S(1)} %reshape.77, bf16[1,256,256]{2,1,0:T(8,128)(2,1)} %neg.30), kind=kLoop, calls=%fused_computation.41 | loop fusion | flops 2097152 | bytes 917504 | tf_op jit(solution)/shard_map/concatenate | solution.py:148
  50.1 0.0 copy-done.2
  50.1 0.0 copy-done.3
  50.1 0.8 maximum_maximum_fusion.1.w2_ref
  51.0 0.8 pad_maximum_fusion.1.fw_ref
  51.8 2.3 %multiply_convert_fusion.1 = (bf16[256,512]{1,0:T(8,128)(2,1)S(1)}, bf16[256,512]{1,0:T(8,128)(2,1)S(1)}) fusion(f32[256]{0:T(256)S(1)} %fusion.27), kind=kLoop, calls=%fused_computation.46 | loop fusion | flops 2752512 | bytes 525312 | tf_op jit(solution)/shard_map/convert.4
  54.1 1.2 pad_maximum_fusion.2
  55.3 0.8 fusion.25.swap_ref
  56.0 24.2 %all-reduce.3.cloned.1.call-done = (f32[512,512]{1,0:T(8,128)}, f32[512,512]{1,0:T(8,128)}) async-done(((f32[512,512]{1,0:T(8,128)}, f32[512,512]{1,0:T(8,128)}), (f32[512,512]{1,0:T(8,128)}, f32[512,512]{1,0:T(8,128)})) %all-reduce.3.cloned.1.call-update) | async-done | bytes 2097168 | tf_op jit(solution)/shard_map/psum | solution.py:244
  80.2 3.2 %add_rsqrt_fusion = (f32[512,512]{1,0:T(8,128)}, f32[512,512]{1,0:T(8,128)}) fusion(f32[512,512]{1,0:T(8,128)} %get-tuple-element.8, f32[512,512]{1,0:T(8,128)} %get-tuple-element.7), kind=kLoop, calls=%fused_computation.15 | loop fusion | flops 1310720 | bytes 4194304 | tf_op jit(solution)/shard_map/rsqrt | solution.py:248
  83.4 27.5 %forward.1.x_ref = bf16[32,512,512]{2,1,0:T(8,128)(2,1)} custom-call(bf16[32,512,512]{2,1,0:T(8,128)(2,1)} %x_ref.3, f32[512,512]{1,0:T(8,128)} %get-tuple-element.10.mean_ref, f32[512,512]{1,0:T(8,128)} %get-tuple-element.9.rstd_ref, f32[32]{0:T(128)} %dynamic_slice.15.gain_ref, f32[32]{0:T(128)} %dynamic_slice.16.shift_ref, ...), custom_call_target="tpu_custom_call" | custom-call | flops 17179869184 | bytes 33554432 | tf_op jit(solution)/shard_map/forward/pallas_call | solution.py:272
  110.9 28.1 %mix.1.s_ref = bf16[32,512,512]{2,1,0:T(8,128)(2,1)} custom-call(bf16[32,512,512]{2,1,0:T(8,128)(2,1)} %forward.1.x_ref, bf16[1,512,512]{2,1,0:T(8,128)(2,1)} %maximum_maximum_fusion.w1_ref, bf16[1,512,512]{2,1,0:T(8,128)(2,1)} %maximum_maximum_fusion.1.w2_ref, f32[1,512,1]{2,1,0:T(8,128)} %broadcast_in_dim.27.bias_ref), custom_call_target="tpu_custom_call" | custom-call | flops 8589934592 | bytes 33554432 | tf_op jit(solution)/shard_map/mix/pallas_call | solution.py:293
  139.0 31.8 %backward.1 = bf16[32,512,512]{2,1,0:T(8,128)(2,1)} custom-call(bf16[32,512,512]{2,1,0:T(8,128)(2,1)} %x_ref.3, bf16[32,512,512]{2,1,0:T(8,128)(2,1)} %mix.1.s_ref, bf16[512,512]{1,0:T(8,128)(2,1)} %get-tuple-element.25.bh_ref, bf16[256,256]{1,0:T(8,128)(2,1)} %fusion.25.swap_ref, bf16[512,512]{1,0:T(8,128)(2,1)} %get-tuple-element.26.iw_ref), custom_call_target="tpu_custom_call" | custom-call | flops 17179869184 | bytes 33554432 | tf_op jit(solution)/shard_map/backward/pallas_call | solution.py:310
  170.8 0.0 copy-done.1
  (8 shorter events, 0.0 us)
Async XLA Ops:
  6.5 39.7 %copy-start = (f32[2,256]{1,0:T(2,128)S(1)}, f32[2,256]{1,0:T(2,128)}, u32[]{:S(2)}) copy-start(f32[2,256]{1,0:T(2,128)} %param.11) | copy-start | bytes 6148
  6.5 73.7 %all-reduce.3.cloned.1.call-start = ((), (), s32[]{:S(2)}) async-start(), calls=%async_computation | async-start | bytes 4194304 | tf_op jit(solution)/shard_map/psum | solution.py:244
  36.6 8.3 %copy-start.4 = (f32[256]{0:T(256)S(1)}, f32[256]{0:T(256)}, u32[]{:S(2)}) copy-start(f32[256]{0:T(256)} %param.7) | copy-start | bytes 3076
  36.6 9.0 %copy-start.5 = (f32[256]{0:T(256)S(1)}, f32[256]{0:T(256)}, u32[]{:S(2)}) copy-start(f32[256]{0:T(256)} %param.8) | copy-start | bytes 3076
  45.0 5.2 %copy-start.2 = (bf16[1,256,256]{2,1,0:T(8,128)(2,1)S(1)}, bf16[1,256,256]{2,1,0:T(8,128)(2,1)}, u32[]{:S(2)}) copy-start(bf16[1,256,256]{2,1,0:T(8,128)(2,1)} %reshape.79) | copy-start | bytes 393220
  45.0 5.2 %copy-start.3 = (bf16[1,256,256]{2,1,0:T(8,128)(2,1)S(1)}, bf16[1,256,256]{2,1,0:T(8,128)(2,1)}, u32[]{:S(2)}) copy-start(bf16[1,256,256]{2,1,0:T(8,128)(2,1)} %neg.31) | copy-start | bytes 393220
  139.0 31.8 %copy-start.1 = (f32[2,256]{1,0:T(2,128)S(1)}, f32[2,256]{1,0:T(2,128)}, u32[]{:S(2)}) copy-start(f32[2,256]{1,0:T(2,128)} %param.11) | copy-start | bytes 6148
Sparse Core Ops, SparseCore 0:
  15.6 64.5 all-reduce.2

commit v2 on v1

--- a/solution.py
+++ b/solution.py
@@ -1,7 +1,9 @@
+import functools
 import math
 
 import jax
 import jax.numpy as jnp
+import numpy as np
 from jax import lax
 from jax.experimental import pallas as pl
 from jax.experimental.pallas import tpu as pltpu
@@ -123,32 +125,154 @@
 SUB = 8
 
 
-def half_tables(cos_h, sin_h):
-    rows = cos_h.shape[0]
-    mid = rows // 2
-    low = jnp.concatenate([cos_h[:mid], cos_h[mid : mid + 1], sin_h[1:mid]], axis=0)
-    picked = jnp.arange(mid, dtype=jnp.int32)
-    swap = (jnp.where(picked == 0, 0, mid - picked)[:, None] == picked[None, :]).astype(
+def constant_tables(rows, cols):
+    half, mid = cols // 2, rows // 2
+    wave = lambda f, left, right, period: f(
+        (left[:, None] * right[None, :] % period).astype(np.float32)
+        * np.float32(2.0 * math.pi / period)
+    ) * np.float32(1.0 / math.sqrt(period))
+    col, mode = np.arange(cols), np.arange(half)
+    fwd_w = np.concatenate(
+        [wave(np.cos, col, mode, cols), -wave(np.sin, col, mode, cols)], axis=1
+    )
+    weight_k = np.where(mode == 0, 1.0, 2.0).astype(np.float32)[:, None]
+    inv_w = np.concatenate(
+        [
+            wave(np.cos, mode, col, cols) * weight_k,
+            -wave(np.sin, mode, col, cols) * weight_k,
+        ],
+        axis=0,
+    )
+    row = np.arange(rows)
+    cos_h, sin_h = wave(np.cos, row, row, rows), wave(np.sin, row, row, rows)
+    low = np.concatenate([cos_h[: mid + 1], sin_h[1:mid]], axis=0)
+    order = np.concatenate([row[: mid + 1], row[mid + 1 :][::-1]])
+    swap = np.zeros((mid, mid), np.float32)
+    swap[row[:mid], (mid - row[:mid]) % mid] = 1.0
+    return tuple(t.astype(jnp.bfloat16) for t in (fwd_w, inv_w, low, low[:, order], swap))
+
+
+def pair_weight(weight):
+    real, imag = weight[0], weight[1]
+    return jnp.concatenate(
+        [jnp.concatenate([real, imag], axis=2), jnp.concatenate([-imag, real], axis=2)], axis=1
+    )
+
+
+def spread_weight(weight):
+    size = weight.shape[0]
+    rows = lax.broadcasted_iota(jnp.int32, (size * SUB, size), 0)
+    cols = lax.broadcasted_iota(jnp.int32, (size * SUB, size), 1)
+    repeat = jnp.where((rows >= cols * SUB) & (rows < cols * SUB + SUB), 1.0, 0.0).astype(
         jnp.bfloat16
     )
-    order = lambda t: jnp.concatenate(
-        [t[:, :mid], t[:, mid : mid + 1], t[:, mid + 1 :][:, ::-1]], axis=1
-    )
-    return low, order(low), swap
-
-
-def spread_weight(weight):
-    eye = jnp.eye(SUB, dtype=weight.dtype)
-    real = jnp.einsum("bio,st->bosit", weight[0], eye)
-    imag = jnp.einsum("bio,st->bosit", weight[1], eye)
-    blocks, width = weight.shape[1], weight.shape[2]
-    size = width * SUB
-    real = real.reshape(blocks, size, size)
-    imag = imag.reshape(blocks, size, size)
-    return jnp.concatenate(
-        [jnp.concatenate([real, -imag], axis=2), jnp.concatenate([imag, real], axis=2)],
-        axis=1,
-    )
+    last = (((1,), (1,)), ((), ()))
+    tall = lax.dot_general(repeat, weight, last, preferred_element_type=jnp.float32)
+    full = lax.dot_general(
+        tall.astype(jnp.bfloat16), repeat, last, preferred_element_type=jnp.float32
+    )
+    left = lax.broadcasted_iota(jnp.int32, full.shape, 0)
+    right = lax.broadcasted_iota(jnp.int32, full.shape, 1)
+    return jnp.where(((left ^ right) & (SUB - 1)) == 0, full, 0.0).astype(jnp.bfloat16)
+
+
+def stats_kernel(n, channels, sum_ref, sq_ref, out_ref, near, part, far, s1, r1, s2, r2, s3, r3, s4, r4):
+    me = lax.axis_index("grid")
+    chips = n // 2
+    core, chip = lax.rem(me, 2), lax.div(me, 2)
+    other = 1 - core
+    sibling = chip * 2 + other
+    rows = sum_ref.shape[0]
+    half, piece = rows // 2, rows // n
+
+    def ahead(j):
+        return lax.rem(chip + j, chips)
+
+    def span(c, k):
+        return pl.ds(pl.multiple_of(c * half + k * piece, 8), piece)
+
+    def send(source, target, send_sem, recv_sem, device):
+        copy = pltpu.make_async_remote_copy(
+            src_ref=source,
+            dst_ref=target,
+            send_sem=send_sem,
+            recv_sem=recv_sem,
+            device_id={"grid": device},
+            device_id_type=pl.DeviceIdType.MESH,
+        )
+        copy.start()
+        return copy
+
+    barrier = pltpu.get_barrier_semaphore()
+    for device in [sibling] + [ahead(j) * 2 + core for j in range(1, chips)]:
+        pl.semaphore_signal(
+            barrier, inc=1, device_id={"grid": device}, device_id_type=pl.DeviceIdType.MESH
+        )
+    pl.semaphore_wait(barrier, chips)
+
+    theirs = pl.ds(pl.multiple_of(other * half, 8), half)
+    first = [
+        send(ref.at[theirs], near.at[i], s1.at[i], r1.at[i], sibling)
+        for i, ref in enumerate((sum_ref, sq_ref))
+    ]
+    for copy in first:
+        copy.wait_recv()
+    second = []
+    for j in range(1, chips + 1):
+        k = ahead(j)
+        local = pl.ds(pl.multiple_of(k * piece, 8), piece)
+        for i, ref in enumerate((sum_ref, sq_ref)):
+            part[j - 1, i] = ref[span(core, k)] + near[i, local]
+    for j in range(1, chips):
+        second.append(
+            send(part.at[j - 1], far.at[j - 1], s2.at[j - 1], r2.at[j - 1], ahead(j) * 2 + core)
+        )
+    total_sum, total_sq = part[chips - 1, 0], part[chips - 1, 1]
+    for j in range(1, chips):
+        second[j - 1].wait_recv()
+        total_sum = total_sum + far[j - 1, 0]
+        total_sq = total_sq + far[j - 1, 1]
+    mean = total_sum * (1.0 / channels)
+    mine = span(core, chip)
+    out_ref[0, mine] = mean
+    out_ref[1, mine] = lax.rsqrt(total_sq * (1.0 / channels) - mean * mean + 1e-05)
+    block = out_ref.at[:, mine]
+    third = [
+        send(block, block, s3.at[j - 1], r3.at[j - 1], ahead(j) * 2 + core)
+        for j in range(1, chips)
+    ]
+    fourth = [send(block, block, s4.at[0], r4.at[0], sibling)]
+    for j in range(1, chips):
+        third[j - 1].wait_recv()
+        block = out_ref.at[:, span(core, ahead(chips - j))]
+        fourth.append(send(block, block, s4.at[j], r4.at[j], sibling))
+    for copy in fourth:
+        copy.wait_recv()
+    for copy in first + second + third + fourth:
+        copy.wait_send()
+
+
+def shared_stats(total_sum, total_sq, n, channels):
+    rows, cols = total_sum.shape
+    chips = n // 2
+    vmem = pl.BlockSpec(memory_space=pltpu.VMEM)
+    counts = (2, chips - 1, chips - 1, chips)
+    return pl.pallas_call(
+        functools.partial(stats_kernel, n, channels),
+        out_shape=jax.ShapeDtypeStruct((2, rows, cols), jnp.float32),
+        in_specs=[vmem, vmem],
+        out_specs=vmem,
+        scratch_shapes=[
+            pltpu.VMEM((2, rows // 2, cols), jnp.float32),
+            pltpu.VMEM((chips, 2, rows // n, cols), jnp.float32),
+            pltpu.VMEM((chips - 1, 2, rows // n, cols), jnp.float32),
+        ]
+        + [pltpu.SemaphoreType.DMA((c,)) for c in counts for _ in range(2)],
+        compiler_params=pltpu.CompilerParams(
+            collective_id=0, has_side_effects=True, vmem_limit_bytes=32 * 1024 * 1024
+        ),
+        name="stats",
+    )(total_sum, total_sq)
 
 
 def split_rows(total, sign):
@@ -168,7 +292,7 @@
     return plus, minus
 
 
-def forward_kernel(x_ref, mean_ref, rstd_ref, gain_ref, shift_ref, fw_ref, fh_ref, out_ref):
+def forward_kernel(x_ref, stats_ref, gain_ref, shift_ref, fw_ref, fh_ref, out_ref):
     count, rows, cols = x_ref.shape
     mid, half = rows // 2, cols // 2
     step = pl.program_id(0)
@@ -176,7 +300,7 @@
         gain = gain_ref[step * count + n]
         shift = shift_ref[step * count + n]
         values = x_ref[n].astype(jnp.float32)
-        normed = ((values - mean_ref[...]) * rstd_ref[...] * gain + shift).astype(jnp.bfloat16)
+        normed = ((values - stats_ref[0]) * stats_ref[1] * gain + shift).astype(jnp.bfloat16)
         along = jnp.dot(normed, fw_ref[...], preferred_element_type=jnp.float32).astype(
             jnp.bfloat16
         )
@@ -189,7 +313,12 @@
                 ].astype(jnp.bfloat16)
 
 
-def mix_kernel(x_ref, w1_ref, w2_ref, bias_ref, out_ref):
+def mix_kernel(x_ref, first_ref, second_ref, bias_ref, out_ref, w1_ref, w2_ref):
+    @pl.when(pl.program_id(1) == 0)
+    def _():
+        w1_ref[...] = spread_weight(first_ref[0])
+        w2_ref[...] = spread_weight(second_ref[0])
+
     width, depth, cols = x_ref.shape
     half = cols // 2
     size = width * SUB
@@ -200,9 +329,9 @@
         for s in range(2):
             flat = values[:, s * SUB : (s + 1) * SUB, :].reshape(size, cols).astype(jnp.bfloat16)
             both = jnp.concatenate([flat[:, :half], flat[:, half:]], axis=0)
-            hid = jnp.dot(w1_ref[0], both, preferred_element_type=jnp.float32)
+            hid = jnp.dot(w1_ref[...], both, preferred_element_type=jnp.float32)
             hid = jnp.maximum(hid + bias_ref[0], 0.0).astype(jnp.bfloat16)
-            mixed = shrink(jnp.dot(w2_ref[0], hid, preferred_element_type=jnp.float32))
+            mixed = shrink(jnp.dot(w2_ref[...], hid, preferred_element_type=jnp.float32))
             parts.append(mixed.reshape(2, width, SUB, half))
         for side in range(2):
             out_ref[:, base : base + 2 * SUB, side * half : (side + 1) * half] = (
@@ -241,19 +370,16 @@
     channels = local_ch * groups
     own_blocks = local_ch // width
     values = fields.astype(jnp.float32)
-    total_sum, total_sq = lax.psum(
-        (jnp.sum(values, axis=0), jnp.sum(values * values, axis=0)), "grid"
-    )
-    mean = total_sum / channels
-    rstd = lax.rsqrt(total_sq / channels - mean * mean + 1e-05)
-    fwd_w, inv_w, cos_h, sin_h = tables(rows, cols)
-    low, ordered, swap = half_tables(cos_h, sin_h)
+    stats = shared_stats(
+        jnp.sum(values, axis=0), jnp.sum(values * values, axis=0), groups, channels
+    )
+    fwd_w, inv_w, low, ordered, swap = (jnp.asarray(t) for t in constant_tables(rows, cols))
     place = lax.axis_index("grid")
     take = lambda a, size, axis: lax.dynamic_slice_in_dim(a, place * size, size, axis)
     gain_own = take(norm_gain, local_ch, 0)
     shift_own = take(norm_shift, local_ch, 0)
-    first_own = spread_weight(take(first_weight, own_blocks, 1))
-    second_own = spread_weight(take(second_weight, own_blocks, 1))
+    first_own = pair_weight(take(first_weight, own_blocks, 1))
+    second_own = pair_weight(take(second_weight, own_blocks, 1))
     bias_own = take(first_bias, local_ch, 1).reshape(2, own_blocks, width)
     bias_own = jnp.repeat(
         bias_own.transpose(1, 0, 2).reshape(own_blocks, 2 * width, 1), SUB, axis=1
@@ -275,8 +401,7 @@
         out_shape=image,
         in_specs=[
             image_spec,
-            whole_spec(mean),
-            whole_spec(rstd),
+            whole_spec(stats),
             smem,
             smem,
             whole_spec(fwd_w),
@@ -286,10 +411,10 @@
         compiler_params=params,
         cost_estimate=cost(2 * fields.size * (rows + cols)),
         name="forward",
-    )(fields, mean, rstd, gain_own, shift_own, fwd_w, low)
+    )(fields, stats, gain_own, shift_own, fwd_w, low)
     depth = 4 * SUB
     mode_spec = pl.BlockSpec((width, depth, cols), lambda b, i: (b, i, 0))
-    weight_spec = pl.BlockSpec((1, size, size), lambda b, i: (b, 0, 0))
+    weight_spec = pl.BlockSpec((1, 2 * width, 2 * width), lambda b, i: (b, 0, 0))
     mixed = pl.pallas_call(
         mix_kernel,
         grid=(own_blocks, rows // depth),
@@ -301,6 +426,7 @@
             pl.BlockSpec((1, size, 1), lambda b, i: (b, 0, 0)),
         ],
         out_specs=mode_spec,
+        scratch_shapes=[pltpu.VMEM((size, size), jnp.bfloat16)] * 2,
         compiler_params=pltpu.CompilerParams(
             dimension_semantics=("arbitrary", "arbitrary"), vmem_limit_bytes=60 * 1024 * 1024
         ),
@@ -329,6 +455,8 @@
     local_ch, rows, cols = fields.shape
     whole_blocks = local_ch % first_weight.shape[2] == 0
     tiled = rows % 64 == 0 and cols % 256 == 0 and rows * cols <= 512 * 1024
+    groups = lax.axis_size("grid")
+    tiled = tiled and groups % 2 == 0 and rows % (8 * groups) == 0
     chosen = per_device_local if whole_blocks and tiled else per_device
     return chosen(fields, norm_gain, norm_shift, first_weight, second_weight, first_bias)
 

time: 180 us -> 140 us (0.78)
  Pallas kernels: 87.4 us -> 123 us
  waiting for transfers between devices: 24.2 us -> 0 us
  other arithmetic: 31.7 us -> 9.64 us
  local copies, waits for them, and re-layouts: 20.8 us -> 5.7 us
  between operations: 13.5 us -> 0.03 us
    pallas_call x0 -> x1, Pallas kernels: none -> 34.5 us  [shared_stats(): pl.pallas_call(functools.partial(stats_kernel, n, channels), out_shape=ja...]
    psum x1 -> x0, waiting for transfers between devices: 24.2 us -> none  [per_device_local(): lax.psum((jnp.sum(values, axis=0), jnp.sum(values * values, axis=0)), 'gr...]
    reshape x5 -> x0, local copies, waits for them, and re-layouts: 16.5 us -> none  [the longest x2 8.24 us: spread_weight(): real = real.reshape(blocks, size, size)]
    concatenate x7 -> x2, other arithmetic: 5.86 us -> 1.37 us  [pair_weight(): jnp.concatenate([jnp.concatenate([real, imag], axis=2), jnp.concatenate([...]
    another operation x3 -> x0, other arithmetic: 4.45 us -> none
    convert_element_type x3 -> x0, other arithmetic: 4.35 us -> none  [the longest x1 1.8 us: tables(): cos_h = (jnp.cos(angle_h) * scale_h).astype(jnp.bfloat16)]
    rsqrt x1 -> x0, other arithmetic: 3.18 us -> none  [per_device_local(): rstd = lax.rsqrt(total_sq / channels - mean * mean + 1e-05)]
    transpose x1 -> x0, other arithmetic: 3.07 us -> none  [spread_weight(): imag = jnp.einsum('bio,st->bosit', weight[1], eye)]
  transfers between devices with their start and end apart: 1 -> 0, of which waited for: 1 -> 0; matrix products, arithmetic and copies ran while one was open for 23% -> 0% of each run, Pallas kernels for 0% -> 0%
where the time goes in v2:
time: 140 us; the launch traced here: 138 us
  Pallas kernels  123 us (88%)
  other arithmetic  9.64 us (7%)
  local copies, waits for them, and re-layouts  5.7 us (4%)
    pallas_call x1, Pallas kernels, shared_stats(): pl.pallas_call(functools.partial(stats_kernel, n, channels), out_shape=ja...  34.5 us
    pallas_call x1, Pallas kernels, per_device_local(): pl.pallas_call(backward_kernel, grid=(local_ch // per,), out_shape=image,...  31.7 us
    pallas_call x1, Pallas kernels, per_device_local(): pl.pallas_call(mix_kernel, grid=(own_blocks, rows // depth), out_shape=im...  28.8 us
    pallas_call x1, Pallas kernels, per_device_local(): pl.pallas_call(forward_kernel, grid=(local_ch // per,), out_shape=image,...  27.5 us
    reduce_sum x1, other arithmetic, per_device_local(): jnp.sum(values * values, axis=0)  7.56 us

profile of v2, /device:TPU:0, one launch (start us, length us, event | category | flops | bytes accessed | tf_op | source)
XLA Modules:
  0.0 137.9 jit_solution(1859297356240027753)
XLA Ops:
  0.0 0.0 copy-start
  0.0 1.3 dynamic_slice.15.gain_ref
  1.3 1.3 dynamic_slice.16.shift_ref
  2.6 0.0 copy-done
  2.6 0.1 constant_dynamic-slice_fusion
  2.7 0.1 reshape_transpose_reshape.3
  2.7 0.7 dynamic-slice_bitcast_fusion.1
  3.5 0.7 fusion.1
  4.2 0.7 maximum_maximum_fusion.1.second_ref
  4.9 0.7 maximum_maximum_fusion.first_ref
  5.5 0.1 broadcast_in_dim.5
  5.6 0.8 broadcast_in_dim.7.bias_ref
  6.5 7.6 %fusion = (f32[512,512]{1,0:T(8,128)S(1)}, f32[512,512]{1,0:T(8,128)S(1)}) fusion(bf16[32,512,512]{2,1,0:T(8,128)(2,1)} %x_ref.3), kind=kLoop, calls=%fused_computation.2 | loop fusion | flops 33030144 | bytes 18874368 | tf_op jit(solution)/shard_map/reduce_sum | solution.py:374
  14.0 34.5 %stats.1.stats_ref = f32[2,512,512]{2,1,0:T(8,128)S(1)} custom-call(f32[512,512]{1,0:T(8,128)S(1)} %get-tuple-element.6.sum_ref, f32[512,512]{1,0:T(8,128)S(1)} %get-tuple-element.5.sq_ref), custom_call_target="tpu_custom_call" | custom-call | tf_op jit(solution)/shard_map/stats/pallas_call | solution.py:260
  48.5 0.0 copy-start.2
  48.5 1.3 copy-done.2
  49.8 27.5 %forward.1.x_ref = bf16[32,512,512]{2,1,0:T(8,128)(2,1)} custom-call(bf16[32,512,512]{2,1,0:T(8,128)(2,1)} %x_ref.3, f32[2,512,512]{2,1,0:T(8,128)} %copy-done.2, f32[32]{0:T(128)} %dynamic_slice.15.gain_ref, f32[32]{0:T(128)} %dynamic_slice.16.shift_ref, bf16[512,512]{1,0:T(8,128)(2,1)} %constant.24.clone.fw_ref, bf16[512,512]{1,0:T(8,128)(2,1)} %constant.26.clone.fh_ref), custom_call_target="tpu_custom_call" | custom-call | flops 17179869184 | bytes 33554432 | tf_op jit(solution)/shard_map/forward/pallas_call | solution.py:398
  77.4 0.0 copy-start.1
  77.4 28.8 %mix.1.s_ref = bf16[32,512,512]{2,1,0:T(8,128)(2,1)} custom-call(bf16[32,512,512]{2,1,0:T(8,128)(2,1)} %forward.1.x_ref, bf16[1,64,64]{2,1,0:T(8,128)(2,1)} %maximum_maximum_fusion.first_ref, bf16[1,64,64]{2,1,0:T(8,128)(2,1)} %maximum_maximum_fusion.1.second_ref, f32[1,512,1]{2,1,0:T(8,128)} %broadcast_in_dim.7.bias_ref), custom_call_target="tpu_custom_call" | custom-call | flops 8589934592 | bytes 33554432 | tf_op jit(solution)/shard_map/mix/pallas_call | solution.py:418
  106.2 31.7 %backward.1 = bf16[32,512,512]{2,1,0:T(8,128)(2,1)} custom-call(bf16[32,512,512]{2,1,0:T(8,128)(2,1)} %x_ref.3, bf16[32,512,512]{2,1,0:T(8,128)(2,1)} %mix.1.s_ref, bf16[512,512]{1,0:T(8,128)(2,1)} %constant.27.clone.bh_ref, bf16[256,256]{1,0:T(8,128)(2,1)} %constant.28.clone.swap_ref, bf16[512,512]{1,0:T(8,128)(2,1)} %constant.25.clone.iw_ref), custom_call_target="tpu_custom_call" | custom-call | flops 17179869184 | bytes 33554432 | tf_op jit(solution)/shard_map/backward/pallas_call | solution.py:436
  137.9 0.0 copy-done.1
Async XLA Ops:
  0.0 2.6 %copy-start = (f32[2,256]{1,0:T(2,128)S(1)}, f32[2,256]{1,0:T(2,128)}, u32[]{:S(2)}) copy-start(f32[2,256]{1,0:T(2,128)} %param.16) | copy-start | bytes 6148
  48.5 1.3 copy-start.2
  77.4 60.5 %copy-start.1 = (f32[2,256]{1,0:T(2,128)S(1)}, f32[2,256]{1,0:T(2,128)}, u32[]{:S(2)}) copy-start(f32[2,256]{1,0:T(2,128)} %param.16) | copy-start | bytes 6148

commit v3 on v2

--- a/solution.py
+++ b/solution.py
@@ -150,13 +150,6 @@
     swap = np.zeros((mid, mid), np.float32)
     swap[row[:mid], (mid - row[:mid]) % mid] = 1.0
     return tuple(t.astype(jnp.bfloat16) for t in (fwd_w, inv_w, low, low[:, order], swap))
-
-
-def pair_weight(weight):
-    real, imag = weight[0], weight[1]
-    return jnp.concatenate(
-        [jnp.concatenate([real, imag], axis=2), jnp.concatenate([-imag, real], axis=2)], axis=1
-    )
 
 
 def spread_weight(weight):
@@ -295,10 +288,10 @@
 def forward_kernel(x_ref, stats_ref, gain_ref, shift_ref, fw_ref, fh_ref, out_ref):
     count, rows, cols = x_ref.shape
     mid, half = rows // 2, cols // 2
-    step = pl.program_id(0)
+    start = (lax.axis_index("grid") * pl.num_programs(0) + pl.program_id(0)) * count
     for n in range(count):
-        gain = gain_ref[step * count + n]
-        shift = shift_ref[step * count + n]
+        gain = gain_ref[start + n]
+        shift = shift_ref[start + n]
         values = x_ref[n].astype(jnp.float32)
         normed = ((values - stats_ref[0]) * stats_ref[1] * gain + shift).astype(jnp.bfloat16)
         along = jnp.dot(normed, fw_ref[...], preferred_element_type=jnp.float32).astype(
@@ -313,11 +306,26 @@
                 ].astype(jnp.bfloat16)
 
 
-def mix_kernel(x_ref, first_ref, second_ref, bias_ref, out_ref, w1_ref, w2_ref):
+def mix_kernel(x_ref, first_ref, second_ref, bias_ref, out_ref, w1_ref, w2_ref, b1_ref):
     @pl.when(pl.program_id(1) == 0)
     def _():
-        w1_ref[...] = spread_weight(first_ref[0])
-        w2_ref[...] = spread_weight(second_ref[0])
+        block = lax.axis_index("grid") * pl.num_programs(0) + pl.program_id(0)
+        width = first_ref.shape[2]
+        size = width * SUB
+        for source, target in ((first_ref, w1_ref), (second_ref, w2_ref)):
+            real = spread_weight(source[0, block])
+            imag = spread_weight(source[1, block])
+            target[:size, :size] = real
+            target[:size, size:] = -imag
+            target[size:, :size] = imag
+            target[size:, size:] = real
+        shape = (size, bias_ref.shape[1])
+        first = (lax.broadcasted_iota(jnp.int32, shape, 1) - block * width) * SUB
+        offset = lax.broadcasted_iota(jnp.int32, shape, 0) - first
+        own = (offset >= 0) & (offset < SUB)
+        for side in range(2):
+            picked = jnp.where(own, bias_ref[side : side + 1, :], 0.0)
+            b1_ref[side * size : (side + 1) * size, :] = jnp.sum(picked, axis=1, keepdims=True)
 
     width, depth, cols = x_ref.shape
     half = cols // 2
@@ -330,8 +338,9 @@
             flat = values[:, s * SUB : (s + 1) * SUB, :].reshape(size, cols).astype(jnp.bfloat16)
             both = jnp.concatenate([flat[:, :half], flat[:, half:]], axis=0)
             hid = jnp.dot(w1_ref[...], both, preferred_element_type=jnp.float32)
-            hid = jnp.maximum(hid + bias_ref[0], 0.0).astype(jnp.bfloat16)
-            mixed = shrink(jnp.dot(w2_ref[...], hid, preferred_element_type=jnp.float32))
+            hid = jnp.maximum(hid + b1_ref[...], 0.0).astype(jnp.bfloat16)
+            mixed = jnp.dot(w2_ref[...], hid, preferred_element_type=jnp.float32)
+            mixed = mixed - jnp.clip(mixed, -0.01, 0.01)
             parts.append(mixed.reshape(2, width, SUB, half))
         for side in range(2):
             out_ref[:, base : base + 2 * SUB, side * half : (side + 1) * half] = (
@@ -359,7 +368,7 @@
 
 def whole_spec(array):
     zeros = (0,) * array.ndim
-    return pl.BlockSpec(array.shape, lambda i: zeros)
+    return pl.BlockSpec(array.shape, lambda *_: zeros)
 
 
 def per_device_local(fields, norm_gain, norm_shift, first_weight, second_weight, first_bias):
@@ -374,16 +383,6 @@
         jnp.sum(values, axis=0), jnp.sum(values * values, axis=0), groups, channels
     )
     fwd_w, inv_w, low, ordered, swap = (jnp.asarray(t) for t in constant_tables(rows, cols))
-    place = lax.axis_index("grid")
-    take = lambda a, size, axis: lax.dynamic_slice_in_dim(a, place * size, size, axis)
-    gain_own = take(norm_gain, local_ch, 0)
-    shift_own = take(norm_shift, local_ch, 0)
-    first_own = pair_weight(take(first_weight, own_blocks, 1))
-    second_own = pair_weight(take(second_weight, own_blocks, 1))
-    bias_own = take(first_bias, local_ch, 1).reshape(2, own_blocks, width)
-    bias_own = jnp.repeat(
-        bias_own.transpose(1, 0, 2).reshape(own_blocks, 2 * width, 1), SUB, axis=1
-    )
     size = 2 * width * SUB
     per = 2 if local_ch % 2 == 0 else 1
     params = pltpu.CompilerParams(
@@ -411,28 +410,28 @@
         compiler_params=params,
         cost_estimate=cost(2 * fields.size * (rows + cols)),
         name="forward",
-    )(fields, stats, gain_own, shift_own, fwd_w, low)
+    )(fields, stats, norm_gain, norm_shift, fwd_w, low)
     depth = 4 * SUB
     mode_spec = pl.BlockSpec((width, depth, cols), lambda b, i: (b, i, 0))
-    weight_spec = pl.BlockSpec((1, 2 * width, 2 * width), lambda b, i: (b, 0, 0))
     mixed = pl.pallas_call(
         mix_kernel,
         grid=(own_blocks, rows // depth),
         out_shape=image,
         in_specs=[
             mode_spec,
-            weight_spec,
-            weight_spec,
-            pl.BlockSpec((1, size, 1), lambda b, i: (b, 0, 0)),
+            whole_spec(first_weight),
+            whole_spec(second_weight),
+            whole_spec(first_bias),
         ],
         out_specs=mode_spec,
-        scratch_shapes=[pltpu.VMEM((size, size), jnp.bfloat16)] * 2,
+        scratch_shapes=[pltpu.VMEM((size, size), jnp.bfloat16)] * 2
+        + [pltpu.VMEM((size, 1), jnp.float32)],
         compiler_params=pltpu.CompilerParams(
             dimension_semantics=("arbitrary", "arbitrary"), vmem_limit_bytes=60 * 1024 * 1024
         ),
         cost_estimate=cost(2 * fields.size * size),
         name="mix",
-    )(modes, first_own, second_own, bias_own)
+    )(modes, first_weight, second_weight, first_bias)
     return pl.pallas_call(
         backward_kernel,
         grid=(local_ch // per,),

time: 140 us -> 133 us (0.950)
  local copies, waits for them, and re-layouts: 5.7 us -> 1.34 us
  other arithmetic: 9.64 us -> 7.54 us
    dynamic_slice x3 -> x0, local copies, waits for them, and re-layouts: 2.65 us -> none  [per_device_local(): lax.dynamic_slice_in_dim(a, place * size, size, axis)]
where the time goes in v3:
time: 133 us; the launch traced here: 131 us
  Pallas kernels  122 us (92%)
  other arithmetic  7.54 us (6%)
  local copies, waits for them, and re-layouts  1.34 us (1%)
    pallas_call x1, Pallas kernels, shared_stats(): pl.pallas_call(functools.partial(stats_kernel, n, channels), out_shape=ja...  34.5 us
    pallas_call x1, Pallas kernels, per_device_local(): pl.pallas_call(backward_kernel, grid=(local_ch // per,), out_shape=image,...  31.7 us
    pallas_call x1, Pallas kernels, per_device_local(): pl.pallas_call(mix_kernel, grid=(own_blocks, rows // depth), out_shape=im...  28.4 us
    pallas_call x1, Pallas kernels, per_device_local(): pl.pallas_call(forward_kernel, grid=(local_ch // per,), out_shape=image,...  27.5 us
    reduce_sum x1, other arithmetic, per_device_local(): jnp.sum(values * values, axis=0)  7.54 us

profile of v3, /device:TPU:0, one launch (start us, length us, event | category | flops | bytes accessed | tf_op | source)
XLA Modules:
  0.0 131.0 jit_solution(17769922829689650600)
XLA Ops:
  0.0 7.5 %fusion = (f32[512,512]{1,0:T(8,128)S(1)}, f32[512,512]{1,0:T(8,128)S(1)}) fusion(bf16[32,512,512]{2,1,0:T(8,128)(2,1)} %x_ref.3), kind=kLoop, calls=%fused_computation.2 | loop fusion | flops 33030144 | bytes 18874368 | tf_op jit(solution)/shard_map/reduce_sum | solution.py:383
  7.5 34.5 %stats.1.stats_ref = f32[2,512,512]{2,1,0:T(8,128)S(1)} custom-call(f32[512,512]{1,0:T(8,128)S(1)} %get-tuple-element.6.sum_ref, f32[512,512]{1,0:T(8,128)S(1)} %get-tuple-element.5.sq_ref), custom_call_target="tpu_custom_call" | custom-call | tf_op jit(solution)/shard_map/stats/pallas_call | solution.py:253
  42.0 0.0 copy-start
  42.0 1.3 %copy-done = f32[2,512,512]{2,1,0:T(8,128)} copy-done((f32[2,512,512]{2,1,0:T(8,128)}, f32[2,512,512]{2,1,0:T(8,128)S(1)}, u32[]{:S(2)}) %copy-start) | copy-done | bytes 2097176
  43.4 27.5 %forward.1.x_ref = bf16[32,512,512]{2,1,0:T(8,128)(2,1)} custom-call(bf16[32,512,512]{2,1,0:T(8,128)(2,1)} %x_ref.3, f32[2,512,512]{2,1,0:T(8,128)} %copy-done, f32[256]{0:T(256)} %gain_ref.1, f32[256]{0:T(256)} %shift_ref.1, bf16[512,512]{1,0:T(8,128)(2,1)} %constant.12.clone.fw_ref, bf16[512,512]{1,0:T(8,128)(2,1)} %constant.14.clone.fh_ref), custom_call_target="tpu_custom_call" | custom-call | flops 17179869184 | bytes 33554432 | tf_op jit(solution)/shard_map/forward/pallas_call | solution.py:397
  70.9 28.4 %mix.1.s_ref = bf16[32,512,512]{2,1,0:T(8,128)(2,1)} custom-call(bf16[32,512,512]{2,1,0:T(8,128)(2,1)} %forward.1.x_ref, bf16[2,8,32,32]{3,2,1,0:T(8,128)(2,1)} %first_ref.1, bf16[2,8,32,32]{3,2,1,0:T(8,128)(2,1)} %second_ref.1, f32[2,256]{1,0:T(2,128)} %bias_ref.1), custom_call_target="tpu_custom_call" | custom-call | flops 8589934592 | bytes 33554432 | tf_op jit(solution)/shard_map/mix/pallas_call | solution.py:416
  99.3 31.7 %backward.1 = bf16[32,512,512]{2,1,0:T(8,128)(2,1)} custom-call(bf16[32,512,512]{2,1,0:T(8,128)(2,1)} %x_ref.3, bf16[32,512,512]{2,1,0:T(8,128)(2,1)} %mix.1.s_ref, bf16[512,512]{1,0:T(8,128)(2,1)} %constant.15.clone.bh_ref, bf16[256,256]{1,0:T(8,128)(2,1)} %constant.16.clone.swap_ref, bf16[512,512]{1,0:T(8,128)(2,1)} %constant.13.clone.iw_ref), custom_call_target="tpu_custom_call" | custom-call | flops 17179869184 | bytes 33554432 | tf_op jit(solution)/shard_map/backward/pallas_call | solution.py:435
Async XLA Ops:
  42.0 1.4 %copy-start = (f32[2,512,512]{2,1,0:T(8,128)}, f32[2,512,512]{2,1,0:T(8,128)S(1)}, u32[]{:S(2)}) copy-start(f32[2,512,512]{2,1,0:T(8,128)S(1)} %stats.1.stats_ref) | copy-start | bytes 6291460

commit v4 on v3

--- a/solution.py
+++ b/solution.py
@@ -384,7 +384,7 @@
     )
     fwd_w, inv_w, low, ordered, swap = (jnp.asarray(t) for t in constant_tables(rows, cols))
     size = 2 * width * SUB
-    per = 2 if local_ch % 2 == 0 else 1
+    per = 4 if local_ch % 4 == 0 else 1
     params = pltpu.CompilerParams(
         dimension_semantics=("arbitrary",), vmem_limit_bytes=60 * 1024 * 1024
     )
@@ -411,7 +411,7 @@
         cost_estimate=cost(2 * fields.size * (rows + cols)),
         name="forward",
     )(fields, stats, norm_gain, norm_shift, fwd_w, low)
-    depth = 4 * SUB
+    depth = 8 * SUB
     mode_spec = pl.BlockSpec((width, depth, cols), lambda b, i: (b, i, 0))
     mixed = pl.pallas_call(
         mix_kernel,

time: 133 us -> 123 us (0.925); the launches traced: 131 us -> 123 us
  Pallas kernels: 122 us -> 114 us
    pallas_call x1, Pallas kernels: 28.4 us -> 25 us  [per_device_local(): pl.pallas_call(mix_kernel, grid=(own_blocks, rows // depth), out_shape=im...]
    pallas_call x1, Pallas kernels: 31.7 us -> 29.5 us  [per_device_local(): pl.pallas_call(backward_kernel, grid=(local_ch // per,), out_shape=image,...]
    pallas_call x1, Pallas kernels: 27.5 us -> 25.3 us  [per_device_local(): pl.pallas_call(forward_kernel, grid=(local_ch // per,), out_shape=image,...]
where the time goes in v4:
time: 123 us
  Pallas kernels  114 us (93%)
  other arithmetic  7.54 us (6%)
  local copies, waits for them, and re-layouts  1.34 us (1%)
    pallas_call x1, Pallas kernels, shared_stats(): pl.pallas_call(functools.partial(stats_kernel, n, channels), out_shape=ja...  34.5 us
    pallas_call x1, Pallas kernels, per_device_local(): pl.pallas_call(backward_kernel, grid=(local_ch // per,), out_shape=image,...  29.5 us
    pallas_call x1, Pallas kernels, per_device_local(): pl.pallas_call(forward_kernel, grid=(local_ch // per,), out_shape=image,...  25.3 us
    pallas_call x1, Pallas kernels, per_device_local(): pl.pallas_call(mix_kernel, grid=(own_blocks, rows // depth), out_shape=im...  25 us
    reduce_sum x1, other arithmetic, per_device_local(): jnp.sum(values * values, axis=0)  7.54 us

profile of v4, /device:TPU:0, one launch (start us, length us, event | category | flops | bytes accessed | tf_op | source)
XLA Modules:
  0.0 123.1 jit_solution(13468749125940064587)
XLA Ops:
  0.0 7.5 %fusion = (f32[512,512]{1,0:T(8,128)S(1)}, f32[512,512]{1,0:T(8,128)S(1)}) fusion(bf16[32,512,512]{2,1,0:T(8,128)(2,1)} %x_ref.3), kind=kLoop, calls=%fused_computation.2 | loop fusion | flops 33030144 | bytes 18874368 | tf_op jit(solution)/shard_map/reduce_sum | solution.py:383
  7.5 34.5 %stats.1.stats_ref = f32[2,512,512]{2,1,0:T(8,128)S(1)} custom-call(f32[512,512]{1,0:T(8,128)S(1)} %get-tuple-element.6.sum_ref, f32[512,512]{1,0:T(8,128)S(1)} %get-tuple-element.5.sq_ref), custom_call_target="tpu_custom_call" | custom-call | tf_op jit(solution)/shard_map/stats/pallas_call | solution.py:253
  42.0 0.0 copy-start
  42.0 1.3 %copy-done = f32[2,512,512]{2,1,0:T(8,128)} copy-done((f32[2,512,512]{2,1,0:T(8,128)}, f32[2,512,512]{2,1,0:T(8,128)S(1)}, u32[]{:S(2)}) %copy-start) | copy-done | bytes 2097176
  43.4 25.3 %forward.1.x_ref = bf16[32,512,512]{2,1,0:T(8,128)(2,1)} custom-call(bf16[32,512,512]{2,1,0:T(8,128)(2,1)} %x_ref.3, f32[2,512,512]{2,1,0:T(8,128)} %copy-done, f32[256]{0:T(256)} %gain_ref.1, f32[256]{0:T(256)} %shift_ref.1, bf16[512,512]{1,0:T(8,128)(2,1)} %constant.12.clone.fw_ref, bf16[512,512]{1,0:T(8,128)(2,1)} %constant.14.clone.fh_ref), custom_call_target="tpu_custom_call" | custom-call | flops 17179869184 | bytes 33554432 | tf_op jit(solution)/shard_map/forward/pallas_call | solution.py:397
  68.7 25.0 %mix.1.s_ref = bf16[32,512,512]{2,1,0:T(8,128)(2,1)} custom-call(bf16[32,512,512]{2,1,0:T(8,128)(2,1)} %forward.1.x_ref, bf16[2,8,32,32]{3,2,1,0:T(8,128)(2,1)} %first_ref.1, bf16[2,8,32,32]{3,2,1,0:T(8,128)(2,1)} %second_ref.1, f32[2,256]{1,0:T(2,128)} %bias_ref.1), custom_call_target="tpu_custom_call" | custom-call | flops 8589934592 | bytes 33554432 | tf_op jit(solution)/shard_map/mix/pallas_call | solution.py:416
  93.7 29.5 %backward.1 = bf16[32,512,512]{2,1,0:T(8,128)(2,1)} custom-call(bf16[32,512,512]{2,1,0:T(8,128)(2,1)} %x_ref.3, bf16[32,512,512]{2,1,0:T(8,128)(2,1)} %mix.1.s_ref, bf16[512,512]{1,0:T(8,128)(2,1)} %constant.15.clone.bh_ref, bf16[256,256]{1,0:T(8,128)(2,1)} %constant.16.clone.swap_ref, bf16[512,512]{1,0:T(8,128)(2,1)} %constant.13.clone.iw_ref), custom_call_target="tpu_custom_call" | custom-call | flops 17179869184 | bytes 33554432 | tf_op jit(solution)/shard_map/backward/pallas_call | solution.py:435
Async XLA Ops:
  42.0 1.4 %copy-start = (f32[2,512,512]{2,1,0:T(8,128)}, f32[2,512,512]{2,1,0:T(8,128)S(1)}, u32[]{:S(2)}) copy-start(f32[2,512,512]{2,1,0:T(8,128)S(1)} %stats.1.stats_ref) | copy-start | bytes 6291460
